TPU v7x, 32 devices: a whole 2x2x4 slice. The times are simulated.
32 devices in a mesh: dp: 4 (over y, x), expert: 8 (over z, core).
Axes of the slice: x: 2, y: 2, z: 4, core: 2. Of those that a mesh axis runs over, the one named last changes fastest.
Arguments:
- tokens: bfloat16 [57344, 768], P(('dp', 'expert')), may hold values from -6 to 6
- lengths: int32 [64], P(('dp', 'expert')), may hold values from 448 to 896, as said below
- routes: int32 [57344], P(('dp', 'expert')), may hold values from 0 to 7, as said below
- slots: int32 [57344], P(('dp', 'expert')), may hold values from 0 to 140, as said below
- ln1_gain: bfloat16 [768], P(('dp', 'expert')), may hold values from 0.5 to 1.5
- ln1_bias: bfloat16 [768], P(('dp', 'expert')), may hold values from -3 to 3
- w_qkv: bfloat16 [768, 2304], P(('dp', 'expert')), may hold values from -0.21875 to 0.21875
- w_attn_out: bfloat16 [768, 768], P(('dp', 'expert')), may hold values from -3.5 to 3.5
- ln2_gain: bfloat16 [768], P(('dp', 'expert')), may hold values from 0.5 to 1.5
- ln2_bias: bfloat16 [768], P(('dp', 'expert')), may hold values from -3 to 3
- route_proj: bfloat16 [768, 16], P(('dp', 'expert')), may hold values from -0.15625 to 0.15625
- expert_embed: float32 [8, 16], replicated, may hold values from -4 to 4
- w_in: bfloat16 [8, 768, 3072], P('expert', 'dp'), may hold values from -0.21875 to 0.21875
- w_expert_out: bfloat16 [8, 3072, 768], P('expert', 'dp'), may hold values from -1.5 to 1.5
- out_grad: bfloat16 [57344, 768], P(('dp', 'expert')), may hold values from -6 to 6
Outputs:
- output: bfloat16 [57344, 768], P(('dp', 'expert'))
- input_grad: bfloat16 [57344, 768], P(('dp', 'expert'))
- ln1_gain_grad: float32 [768], P(('dp', 'expert'))
- ln1_bias_grad: float32 [768], P(('dp', 'expert'))
- w_qkv_grad: float32 [768, 2304], P(('dp', 'expert'))
- w_attn_out_grad: float32 [768, 768], P(('dp', 'expert'))
- ln2_gain_grad: float32 [768], P(('dp', 'expert'))
- ln2_bias_grad: float32 [768], P(('dp', 'expert'))
- route_proj_grad: float32 [768, 16], P(('dp', 'expert'))
- expert_embed_grad: float32 [8, 16], replicated
- w_in_grad: float32 [8, 768, 3072], P('expert', 'dp')
- w_expert_out_grad: float32 [8, 3072, 768], P('expert', 'dp')
Inputs may be any that keep to these rules, and one draw needn't show every extreme that they name: `lengths`: real tokens of a sequence slot; positions from the length on are padding. `routes`: every token, padding too, names one of the 8 experts. Within one sequence slot the tokens of one expert carry the slots 0, 1, 2, ... up to 139 once each as far as they go; every further token of that expert carries 140 and is dropped.
All inputs are finite; a program needn't handle non-finite values.
Results may differ from a plain program's by a relative error of at most 0.023.
Values may be sent and summed in bfloat16 or wider, within the bound.
A program may use at most 384 MiB of HBM per device.

v0:
```python
from functools import partial
import math

import jax
import jax.numpy as jnp
from jax import lax
from jax.sharding import PartitionSpec as P

D = 768
HEADS = 12
HEAD_DIM = 64
FF = 3072
ROUTE = 16
SEQ = 896
MB = 2


norm_eps = 1e-05
route_scale = 3.0
neg_big = -1e30
group_heads = 4
highest = lax.Precision.HIGHEST


def layer_norm(values, gain_vec, shift_vec):
    center = values - jnp.mean(values, axis=-1, keepdims=True)
    spread = jnp.mean(center * center, axis=-1, keepdims=True)
    return center * lax.rsqrt(spread + norm_eps) * gain_vec + shift_vec


def unit_rows(values):
    norm_of = jnp.sqrt(jnp.sum(values * values, axis=-1, keepdims=True))
    return values / jnp.maximum(norm_of, 1.0)


def gelu_exact(values):
    return jax.nn.gelu(values, approximate=False)


def router_gate(picked, router_rows, embed_rows):
    logits = route_scale * jnp.dot(
        unit_rows(router_rows), unit_rows(embed_rows).T, precision=highest
    )
    chances = jax.nn.softmax(logits, axis=-1)
    return jnp.sum(chances * picked, axis=-1)


def head_block(joined_qkv, group_at):
    head_span = group_heads * HEAD_DIM
    start_col = group_at * head_span
    row_shape = (joined_qkv.shape[0], group_heads, HEAD_DIM)
    queries = joined_qkv[:, start_col : start_col + head_span].reshape(row_shape)
    key_rows = joined_qkv[:, D + start_col : D + start_col + head_span].reshape(row_shape)
    value_rows = joined_qkv[:, 2 * D + start_col : 2 * D + start_col + head_span].reshape(row_shape)
    return (queries, key_rows, value_rows)


def send_expert_grads(grad_win, grad_wout):
    return (
        lax.psum_scatter(
            grad_win[None].astype(jnp.bfloat16), "dp", scatter_dimension=1, tiled=True
        ).astype(jnp.float32),
        lax.psum_scatter(
            grad_wout[None].astype(jnp.bfloat16), "dp", scatter_dimension=1, tiled=True
        ).astype(jnp.float32),
    )


def per_device(
    tokens,
    lengths,
    routes,
    slots,
    ln1_gain,
    ln1_bias,
    w_qkv,
    w_attn_out,
    ln2_gain,
    ln2_bias,
    route_proj,
    expert_embed,
    w_in,
    w_expert_out,
    out_grad,
):
    experts = expert_embed.shape[0]
    capacity = 5 * SEQ // (4 * experts)
    slot_cols = experts * capacity
    score_scale = 1.0 / math.sqrt(HEAD_DIM)
    head_span = group_heads * HEAD_DIM
    places = jnp.arange(SEQ, dtype=jnp.int32)
    columns = jnp.arange(slot_cols, dtype=jnp.int32)
    expert_ids = jnp.arange(experts, dtype=jnp.int32)

    def dense_set():
        return (
            lax.all_gather(ln1_gain, ("dp", "expert"), axis=0, tiled=True),
            lax.all_gather(ln1_bias, ("dp", "expert"), axis=0, tiled=True),
            lax.all_gather(w_qkv, ("dp", "expert"), axis=0, tiled=True),
            lax.all_gather(w_attn_out, ("dp", "expert"), axis=0, tiled=True),
            lax.all_gather(ln2_gain, ("dp", "expert"), axis=0, tiled=True),
            lax.all_gather(ln2_bias, ("dp", "expert"), axis=0, tiled=True),
            lax.all_gather(route_proj, ("dp", "expert"), axis=0, tiled=True),
        )

    def expert_set():
        return (
            lax.all_gather(w_in, "dp", axis=1, tiled=True),
            lax.all_gather(w_expert_out, "dp", axis=1, tiled=True),
        )

    grad_gain_one = jnp.zeros((D,), jnp.float32)
    grad_shift_one = jnp.zeros((D,), jnp.float32)
    grad_qkv = jnp.zeros((D, 3 * D), jnp.float32)
    grad_attn = jnp.zeros((D, D), jnp.float32)
    grad_gain_two = jnp.zeros((D,), jnp.float32)
    grad_shift_two = jnp.zeros((D,), jnp.float32)
    grad_proj = jnp.zeros((D, ROUTE), jnp.float32)
    grad_embed = jnp.zeros(expert_embed.shape, jnp.float32)
    grad_win = jnp.zeros((D, FF), jnp.float32)
    grad_wout = jnp.zeros((FF, D), jnp.float32)
    expert_grads = None
    outputs = []
    in_grads = []
    for micro_at in range(MB):
        dense_now = dense_set()
        expert_now = expert_set()
        gain_one, shift_one, qkv_full, attn_full, gain_two, shift_two, proj_full = dense_now
        win_full = expert_now[0][0]
        wout_full = expert_now[1][0]
        span_lo = micro_at * SEQ
        inputs = tokens[span_lo : span_lo + SEQ].astype(jnp.float32)
        length = lengths[micro_at]
        routed = routes[span_lo : span_lo + SEQ]
        slot_of = slots[span_lo : span_lo + SEQ]
        normed_one, back_one = jax.vjp(
            layer_norm, inputs, gain_one.astype(jnp.float32), shift_one.astype(jnp.float32)
        )
        low_one = normed_one.astype(jnp.bfloat16)
        joined_qkv = jnp.dot(low_one, qkv_full, preferred_element_type=jnp.float32).astype(
            jnp.bfloat16
        )
        allowed = (places[None, :] <= places[:, None]) & (places[None, :] < length)
        mixed_parts = []
        lse_parts = []
        for group_at in range(HEADS // group_heads):
            queries, key_rows, value_rows = head_block(joined_qkv, group_at)
            scores = (
                jnp.einsum("qhd,khd->hqk", queries, key_rows, preferred_element_type=jnp.float32)
                * score_scale
            )
            scores = jnp.where(allowed[None], scores, neg_big)
            row_top = jnp.max(scores, axis=-1, keepdims=True)
            exponent = jnp.exp(scores - row_top)
            row_total = jnp.sum(exponent, axis=-1, keepdims=True)
            softmaxed = (exponent / row_total).astype(jnp.bfloat16)
            lse_parts.append(row_top + jnp.log(row_total))
            mixed_parts.append(
                jnp.einsum(
                    "hqk,khd->qhd", softmaxed, value_rows, preferred_element_type=jnp.float32
                ).reshape(SEQ, head_span)
            )
        mixed_heads = jnp.concatenate(mixed_parts, axis=1).astype(jnp.bfloat16)
        hidden_res = inputs + jnp.dot(mixed_heads, attn_full, preferred_element_type=jnp.float32)
        normed_two, back_two = jax.vjp(
            layer_norm, hidden_res, gain_two.astype(jnp.float32), shift_two.astype(jnp.float32)
        )
        low_two = normed_two.astype(jnp.bfloat16)
        router_rows = jnp.dot(low_two, proj_full, preferred_element_type=jnp.float32)
        picked = (routed[:, None] == expert_ids[None, :]).astype(jnp.float32)
        gate_val, back_gate = jax.vjp(partial(router_gate, picked), router_rows, expert_embed)
        live_rows = (places < length) & (slot_of < capacity)
        target = routed * capacity + slot_of
        slot_table = ((target[:, None] == columns[None, :]) & live_rows[:, None]).astype(
            jnp.bfloat16
        )
        sent_rows = (
            jnp.einsum("tc,td->cd", slot_table, low_two, preferred_element_type=jnp.float32)
            .astype(jnp.bfloat16)
            .reshape(experts, capacity, D)
        )
        arrived = lax.all_to_all(sent_rows, "expert", split_axis=0, concat_axis=0, tiled=True)
        pre_act = jnp.einsum("scd,df->scf", arrived, win_full, preferred_element_type=jnp.float32)
        inner_act = gelu_exact(pre_act).astype(jnp.bfloat16)
        returned = jnp.einsum(
            "scf,fd->scd", inner_act, wout_full, preferred_element_type=jnp.float32
        ).astype(jnp.bfloat16)
        arrived, pre_act, inner_act, returned = (arrived, pre_act, inner_act, returned)
        back_home = lax.all_to_all(returned, "expert", split_axis=0, concat_axis=0, tiled=True)
        chosen = jnp.dot(
            slot_table, back_home.reshape(slot_cols, D), preferred_element_type=jnp.float32
        )
        outputs.append((hidden_res + gate_val[:, None] * chosen).astype(jnp.bfloat16))
        dense_back = dense_set()
        expert_back = expert_set()
        qkv_back = dense_back[2]
        attn_back = dense_back[3]
        proj_back = dense_back[6]
        win_back = expert_back[0][0]
        wout_back = expert_back[1][0]
        upstream = out_grad[span_lo : span_lo + SEQ].astype(jnp.float32)
        d_gate = jnp.sum(upstream * chosen, axis=-1)
        d_home = (
            jnp.einsum(
                "tc,td->cd",
                slot_table,
                (gate_val[:, None] * upstream).astype(jnp.bfloat16),
                preferred_element_type=jnp.float32,
            )
            .astype(jnp.bfloat16)
            .reshape(experts, capacity, D)
        )
        d_returned = lax.all_to_all(d_home, "expert", split_axis=0, concat_axis=0, tiled=True)
        d_inner = jnp.einsum(
            "scd,fd->scf", d_returned, wout_back, preferred_element_type=jnp.float32
        )
        _, gelu_back = jax.vjp(gelu_exact, pre_act)
        d_pre = gelu_back(d_inner)[0].astype(jnp.bfloat16)
        grad_wout = grad_wout + jnp.einsum(
            "scf,scd->fd", inner_act, d_returned, preferred_element_type=jnp.float32
        )
        grad_win = grad_win + jnp.einsum(
            "scd,scf->df", arrived, d_pre, preferred_element_type=jnp.float32
        )
        d_sent = jnp.einsum(
            "scf,df->scd", d_pre, win_back, preferred_element_type=jnp.float32
        ).astype(jnp.bfloat16)
        d_arrived = lax.all_to_all(d_sent, "expert", split_axis=0, concat_axis=0, tiled=True)
        d_rows, d_embed = back_gate(d_gate)
        grad_embed = grad_embed + d_embed
        d_router = d_rows.astype(jnp.bfloat16)
        grad_proj = grad_proj + jnp.einsum(
            "td,tr->dr", low_two, d_router, preferred_element_type=jnp.float32
        )
        d_normed_two = jnp.einsum(
            "tr,dr->td", d_router, proj_back, preferred_element_type=jnp.float32
        )
        d_normed_two = d_normed_two + jnp.dot(
            slot_table, d_arrived.reshape(slot_cols, D), preferred_element_type=jnp.float32
        )
        d_from_two, d_gain_two, d_shift_two = back_two(d_normed_two)
        grad_gain_two = grad_gain_two + d_gain_two
        grad_shift_two = grad_shift_two + d_shift_two
        d_hidden = upstream + d_from_two
        d_branch = d_hidden.astype(jnp.bfloat16)
        grad_attn = grad_attn + jnp.einsum(
            "tc,td->cd", mixed_heads, d_branch, preferred_element_type=jnp.float32
        )
        d_mixed = jnp.einsum(
            "td,cd->tc", d_branch, attn_back, preferred_element_type=jnp.float32
        ).astype(jnp.bfloat16)
        query_grads = []
        key_grads = []
        value_grads = []
        for group_at in range(HEADS // group_heads):
            queries, key_rows, value_rows = head_block(joined_qkv, group_at)
            d_heads = d_mixed[:, group_at * head_span : (group_at + 1) * head_span].reshape(
                SEQ, group_heads, HEAD_DIM
            )
            scores = (
                jnp.einsum("qhd,khd->hqk", queries, key_rows, preferred_element_type=jnp.float32)
                * score_scale
            )
            scores = jnp.where(allowed[None], scores, neg_big)
            softmaxed = jnp.exp(scores - lse_parts[group_at])
            d_probs = jnp.einsum(
                "qhd,khd->hqk", d_heads, value_rows, preferred_element_type=jnp.float32
            )
            d_scores = (
                softmaxed * (d_probs - jnp.sum(softmaxed * d_probs, axis=-1, keepdims=True))
            ).astype(jnp.bfloat16)
            query_grads.append(
                (
                    jnp.einsum(
                        "hqk,khd->qhd", d_scores, key_rows, preferred_element_type=jnp.float32
                    )
                    * score_scale
                ).reshape(SEQ, head_span)
            )
            key_grads.append(
                (
                    jnp.einsum(
                        "hqk,qhd->khd", d_scores, queries, preferred_element_type=jnp.float32
                    )
                    * score_scale
                ).reshape(SEQ, head_span)
            )
            value_grads.append(
                jnp.einsum(
                    "hqk,qhd->khd",
                    softmaxed.astype(jnp.bfloat16),
                    d_heads,
                    preferred_element_type=jnp.float32,
                ).reshape(SEQ, head_span)
            )
        d_joined = jnp.concatenate(query_grads + key_grads + value_grads, axis=1).astype(
            jnp.bfloat16
        )
        grad_qkv = grad_qkv + jnp.einsum(
            "tc,td->cd", low_one, d_joined, preferred_element_type=jnp.float32
        )
        d_normed_one = jnp.einsum(
            "td,cd->tc", d_joined, qkv_back, preferred_element_type=jnp.float32
        )
        d_from_one, d_gain_one, d_shift_one = back_one(d_normed_one)
        grad_gain_one = grad_gain_one + d_gain_one
        grad_shift_one = grad_shift_one + d_shift_one
        in_grads.append((d_hidden + d_from_one).astype(jnp.bfloat16))
    dense_grads = (
        lax.psum_scatter(grad_gain_one, ("dp", "expert"), scatter_dimension=0, tiled=True),
        lax.psum_scatter(grad_shift_one, ("dp", "expert"), scatter_dimension=0, tiled=True),
        lax.psum_scatter(grad_qkv, ("dp", "expert"), scatter_dimension=0, tiled=True),
        lax.psum_scatter(grad_attn, ("dp", "expert"), scatter_dimension=0, tiled=True),
        lax.psum_scatter(grad_gain_two, ("dp", "expert"), scatter_dimension=0, tiled=True),
        lax.psum_scatter(grad_shift_two, ("dp", "expert"), scatter_dimension=0, tiled=True),
        lax.psum_scatter(grad_proj, ("dp", "expert"), scatter_dimension=0, tiled=True),
    )
    expert_grads = send_expert_grads(grad_win, grad_wout)
    embed_grad = lax.psum(grad_embed, ("dp", "expert"))
    return (
        jnp.concatenate(outputs, axis=0),
        jnp.concatenate(in_grads, axis=0),
        dense_grads[0],
        dense_grads[1],
        dense_grads[2],
        dense_grads[3],
        dense_grads[4],
        dense_grads[5],
        dense_grads[6],
        embed_grad,
        expert_grads[0],
        expert_grads[1],
    )


def solution(mesh):
    placed = (
        P(("dp", "expert"), None),
        P(("dp", "expert")),
        P(("dp", "expert")),
        P(("dp", "expert")),
        P(("dp", "expert")),
        P(("dp", "expert")),
        P(("dp", "expert"), None),
        P(("dp", "expert"), None),
        P(("dp", "expert")),
        P(("dp", "expert")),
        P(("dp", "expert"), None),
        P(),
        P("expert", "dp", None),
        P("expert", "dp", None),
        P(("dp", "expert"), None),
    )
    return jax.shard_map(
        per_device,
        mesh=mesh,
        in_specs=placed,
        out_specs=(
            P(("dp", "expert"), None),
            P(("dp", "expert"), None),
            P(("dp", "expert")),
            P(("dp", "expert")),
            P(("dp", "expert"), None),
            P(("dp", "expert"), None),
            P(("dp", "expert")),
            P(("dp", "expert")),
            P(("dp", "expert"), None),
            P(),
            P("expert", "dp", None),
            P("expert", "dp", None),
        ),
        check_vma=False,
    )
```

profile of v0, /device:TPU:0, one launch (start us, length us, event | category | flops | bytes accessed | tf_op | source)
XLA Modules:
  0.0 1102.6 jit_solution(16617105235283831170)
XLA Ops:
  18.0 42.3 %all-reduce.10 = (bf16[768]{0:T(1024)(128)(2,1)S(1)}, bf16[768]{0:T(1024)(128)(2,1)S(1)}, bf16[768]{0:T(1024)(128)(2,1)S(1)}, bf16[768]{0:T(1024)(128)(2,1)S(1)}) all-reduce(bf16[768]{0:T(1024)(128)(2,1)S(1)} %dynamic-update-slice.1, bf16[768]{0:T(1024)(128)(2,1)S(1)} %dynamic-update-slice, ...), channel_id=1, replica_groups=mesh['dp'=4,'expert'=8] {'dp','expert'}, use_global_device_ids=true, to_apply=%add.1 | all-reduce | flops 3072 | bytes 12288
  75.5 5.6 convolution_convert_fusion
  95.7 5.6 convolution_convert_fusion.1
  187.3 7.6 fusion.179
  213.0 71.4 %all-gather = bf16[32,24,16]{1,2,0:T(8,128)(2,1)S(1)} all-gather(bf16[1,24,16]{1,2,0:T(8,128)(2,1)S(1)} %bitcast.353), channel_id=1, replica_groups=mesh['dp'=4,'expert'=8] {'dp','expert'}, dimensions={0}, use_global_device_ids=true | all-gather | bytes 25344 | tf_op jit(solution)/shard_map/all_gather | solution.py:103
  304.1 11.7 %fusion.88 = (u8[140,3072]{1,0:T(8,128)(4,1)S(1)}, u8[140,3072]{1,0:T(8,128)(4,1)S(1)}, f32[8,140,3072]{2,1,0:T(8,128)S(1)}) fusion(bf16[8,140,768]{2,1,0:T(8,128)(2,1)} %all-to-all-done, bf16[1,768,3072]{2,1,0:T(8,128)(2,1)} %all-gather.10.cloned.1.call-done), kind=kOutput, calls=%fused_computation.166 | convolution fusion | flops 5328691200 | bytes 21061632 | tf_op jit(solution)/shard_map/scd,df->scf/dot_general | solution.py:183
  320.8 32.6 %multiply_convert_fusion.1 = (bf16[8,140,3072]{2,1,0:T(8,128)(2,1)}, f32[8,140,3072]{2,1,0:T(8,128)}) fusion(f32[8,140,3072]{2,1,0:T(8,128)S(1)} %get-tuple-element.159, u8[140,3072]{1,0:T(8,128)(4,1)S(1)} %get-tuple-element.49, u8[140,3072]{1,0:T(8,128)(4,1)S(1)} %get-tuple-element.48), kind=kLoop, calls=%fused_computation.28 | loop fusion | flops 240844800 | bytes 35266560 | tf_op jit(solution)/shard_map/convert_element_type | solution.py:184
  353.4 10.1 fusion.136
  368.9 11.2 %fusion.89 = (u8[140,3072]{1,0:T(8,128)(4,1)S(1)}, u8[140,3072]{1,0:T(8,128)(4,1)S(1)}, f32[8,140,3072]{2,1,0:T(8,128)S(1)}) fusion(bf16[8,140,768]{2,1,0:T(8,128)(2,1)S(1)} %all-to-all-done.2, bf16[1,768,3072]{2,1,0:T(8,128)(2,1)} %all-gather.10.cloned.1.call-done), kind=kOutput, calls=%fused_computation.167 | convolution fusion | flops 5328691200 | bytes 21061632 | tf_op jit(solution)/shard_map/scd,df->scf/dot_general | solution.py:183
  380.1 32.8 %multiply_convert_fusion = (bf16[8,140,3072]{2,1,0:T(8,128)(2,1)S(1)}, f32[8,140,3072]{2,1,0:T(8,128)}) fusion(f32[8,140,3072]{2,1,0:T(8,128)S(1)} %get-tuple-element.168, u8[140,3072]{1,0:T(8,128)(4,1)S(1)} %get-tuple-element.51, u8[140,3072]{1,0:T(8,128)(4,1)S(1)} %get-tuple-element.50), kind=kLoop, calls=%fused_computation.15 | loop fusion | flops 240844800 | bytes 35266560 | tf_op jit(solution)/shard_map/convert_element_type | solution.py:184
  415.8 9.1 fusion.139
  424.9 5.7 all-to-all-start.3
  443.0 29.7 %all-to-all-done.3 = bf16[8,140,768]{2,1,0:T(8,128)(2,1)} async-done(((bf16[8,140,768]{2,1,0:T(8,128)(2,1)}), bf16[8,140,768]{2,1,0:T(8,128)(2,1)}, u32[]{:S(2)}, u32[]{:S(2)}) %all-to-all-start.3) | async-done | bytes 1720352 | tf_op jit(solution)/shard_map/all_to_all | solution.py:189
  494.4 23.8 %all-to-all-done.4 = bf16[8,140,768]{2,1,0:T(8,128)(2,1)S(1)} async-done(((bf16[8,140,768]{2,1,0:T(8,128)(2,1)}), bf16[8,140,768]{2,1,0:T(8,128)(2,1)S(1)}, u32[]{:S(2)}, u32[]{:S(2)}) %all-to-all-start.4) | async-done | bytes 1720352 | tf_op jit(solution)/shard_map/all_to_all | solution.py:213
  522.7 17.8 %add_convert_fusion.1 = bf16[8,140,3072]{2,1,0:T(8,128)(2,1)} fusion(f32[8,140,3072]{2,1,0:T(8,128)} %get-tuple-element.86, f32[8,140,3072]{2,1,0:T(8,128)} %copy-done.23, bf16[8,140,768]{2,1,0:T(8,128)(2,1)S(1)} %all-to-all-done.4, bf16[1,3072,768]{2,1,0:T(8,128)(2,1)} %all-gather.12.cloned.1.call-done), kind=kOutput, calls=%fused_computation.14 | convolution fusion | flops 5332992000 | bytes 40845312 | tf_op jit(solution)/shard_map/scd,fd->scf/dot_general | solution.py:214
  540.4 10.2 fusion.130
  550.7 10.7 fusion.248
  568.3 12.4 %fusion.65 = bf16[1,3072,768]{2,1,0:T(8,128)(2,1)} fusion(bf16[8,140,3072]{2,1,0:T(8,128)(2,1)} %copy-done.31, bf16[8,140,768]{2,1,0:T(8,128)(2,1)} %all-to-all-done.6, f32[3072,768,1]{1,0,2:T(8,128)} %fusion.248), kind=kOutput, calls=%fused_computation.129 | convolution fusion | flops 5289541632 | bytes 22757376 | tf_op jit(solution)/shard_map/scf,scd->fd/dot_general | solution.py:219
  580.8 19.6 %add_convert_fusion = bf16[8,140,3072]{2,1,0:T(8,128)(2,1)} fusion(f32[8,140,3072]{2,1,0:T(8,128)} %get-tuple-element.88, f32[8,140,3072]{2,1,0:T(8,128)} %copy-done.22, bf16[8,140,768]{2,1,0:T(8,128)(2,1)} %all-to-all-done.6, bf16[1,3072,768]{2,1,0:T(8,128)(2,1)} %all-gather.12.cloned.1.call-done), kind=kOutput, calls=%fused_computation.13 | convolution fusion | flops 5332992000 | bytes 40845312 | tf_op jit(solution)/shard_map/scd,fd->scf/dot_general | solution.py:214
  600.4 10.5 fusion.133
  610.9 11.5 %fusion.247 = f32[768,3072,1]{1,0,2:T(8,128)} fusion(bf16[8,140,768]{2,1,0:T(8,128)(2,1)} %all-to-all-done, bf16[8,140,3072]{2,1,0:T(8,128)(2,1)} %add_convert_fusion.1), kind=kOutput, calls=%fused_computation.416 | convolution fusion | flops 5284823040 | bytes 18038784 | tf_op jit(solution)/shard_map/scd,scf->df/dot_general | solution.py:222
  627.7 12.5 %fusion.64 = bf16[1,768,3072]{2,1,0:T(8,128)(2,1)} fusion(bf16[8,140,768]{2,1,0:T(8,128)(2,1)S(1)} %copy-done.21, bf16[8,140,3072]{2,1,0:T(8,128)(2,1)} %add_convert_fusion, f32[768,3072,1]{1,0,2:T(8,128)} %fusion.247), kind=kOutput, calls=%fused_computation.128 | convolution fusion | flops 5289541632 | bytes 22757376 | tf_op jit(solution)/shard_map/scd,scf->df/dot_general | solution.py:222
  645.1 24.7 %all-to-all-done.7 = bf16[8,140,768]{2,1,0:T(8,128)(2,1)} async-done(((bf16[8,140,768]{2,1,0:T(8,128)(2,1)}), bf16[8,140,768]{2,1,0:T(8,128)(2,1)}, u32[]{:S(2)}, u32[]{:S(2)}) %all-to-all-start.7) | async-done | bytes 1720352 | tf_op jit(solution)/shard_map/all_to_all | solution.py:228
  692.3 6.1 multiply_reduce_fusion.5
  698.4 10.0 multiply_convert_fusion.7
  708.5 5.8 fusion.169
  719.2 5.8 multiply_reduce_fusion.3
  725.1 10.0 multiply_convert_fusion.5
  735.1 5.8 fusion.171
  743.0 5.9 multiply_reduce_fusion.4
  748.8 6.6 multiply_convert_fusion.6
  763.9 5.9 multiply_reduce_fusion.2
  769.7 6.2 multiply_convert_fusion.4
  787.5 11.9 %multiply_reduce_fusion = (f32[4,896]{1,0:T(4,128)S(1)}, f32[4,896,896]{1,2,0:T(8,128)}) fusion(f32[4,896,896]{1,2,0:T(8,128)} %copy-done, f32[4,896]{1,0:T(4,128)S(1)} %copy-done.93, bf16[896,4,64]{0,2,1:T(8,128)(2,1)S(1)} %bitcast.311, bf16[896,4,64]{0,2,1:T(8,128)(2,1)} %bitcast.342), kind=kOutput, calls=%fused_computation.42 | convolution fusion | flops 420672000 | bytes 26636288 | tf_op jit(solution)/shard_map/qhd,khd->hqk/dot_general | solution.py:266
  799.5 10.2 multiply_convert_fusion.2
  809.7 5.9 fusion.177
  820.4 6.0 multiply_reduce_fusion.1
  826.5 10.3 multiply_convert_fusion.3
  836.7 5.9 fusion.176
  850.3 7.8 fusion.157
  861.0 7.6 fusion.154
  879.3 7.1 fusion.163
  890.6 6.2 convolution_add_fusion
  908.5 8.2 fusion.244
  920.0 8.2 fusion.245
  939.1 38.8 %all-reduce.9 = (f32[768]{0:T(1024)S(1)}, f32[768]{0:T(1024)S(1)}, f32[768]{0:T(1024)S(1)}, f32[768]{0:T(1024)S(1)}, f32[768,16]{0,1:T(8,128)S(1)}, /*index=5*/f32[8,16]{1,0:T(8,128)}) all-reduce(f32[768]{0:T(1024)S(1)} %add.230, f32[768]{0:T(1024)S(1)} %add.231, ...), channel_id=2, replica_groups=mesh['dp'=4,'expert'=8] {'dp','expert'}, use_global_device_ids=true, to_apply=%region_51.52.clone | all-reduce | flops 15488 | bytes 123904
  980.3 6.7 add_convert_fusion.3
  996.5 99.1 %reduce-scatter.6.cloned.1.call-done = f32[24,2304]{1,0:T(8,128)} async-done(((f32[768,2304]{1,0:T(8,128)}), f32[24,2304]{1,0:T(8,128)}) %reduce-scatter.6.cloned.1.call-update) | async-done | bytes 221200 | tf_op jit(solution)/shard_map/reduce_scatter | solution.py:312
  (770 shorter events, 347.6 us)
Async XLA Ops:
  7.2 68.3 %all-gather.6.cloned.1.call-start = ((), (), s32[]{:S(2)}) async-start(), calls=%async_computation.12 | async-start | bytes 3649536 | tf_op jit(solution)/shard_map/all_gather | solution.py:99
  7.9 174.1 %all-gather.8.cloned.1.call-start = ((), (), s32[]{:S(2)}) async-start(), calls=%async_computation.13 | async-start | bytes 1216512 | tf_op jit(solution)/shard_map/all_gather | solution.py:100
  8.7 295.4 %all-gather.10.cloned.1.call-start = ((), (), s32[]{:S(2)}) async-start(), calls=%async_computation.14 | async-start | bytes 5898240 | tf_op jit(solution)/shard_map/all_gather | solution.py:108
  69.5 112.5 %copy-start.7 = (bf16[896,768]{0,1:T(8,128)(2,1)}, bf16[896,768]{0,1:T(8,128)(2,1)S(1)}, u32[]{:S(2)}) copy-start(bf16[896,768]{0,1:T(8,128)(2,1)S(1)} %copy.259) | copy-start | bytes 4128772
  90.5 75.7 %copy-start.34 = (bf16[896,256]{0,1:T(8,128)(2,1)}, bf16[896,256]{0,1:T(8,128)(2,1)S(1)}, u32[]{:S(2)}) copy-start(bf16[896,256]{0,1:T(8,128)(2,1)S(1)} %copy.188) | copy-start | bytes 1376260
  201.9 98.0 %copy-start.26 = (bf16[896,768]{0,1:T(8,128)(2,1)}, bf16[896,768]{0,1:T(8,128)(2,1)S(1)}, u32[]{:S(2)}) copy-start(bf16[896,768]{0,1:T(8,128)(2,1)S(1)} %get-tuple-element.125) | copy-start | bytes 4128772
  201.9 229.0 %copy-start.25 = (bf16[896,768]{0,1:T(8,128)(2,1)}, bf16[896,768]{0,1:T(8,128)(2,1)S(1)}, u32[]{:S(2)}) copy-start(bf16[896,768]{0,1:T(8,128)(2,1)S(1)} %get-tuple-element.126) | copy-start | bytes 4128772
  208.1 92.2 %all-to-all-start = ((bf16[8,140,768]{2,1,0:T(8,128)(2,1)}), bf16[8,140,768]{2,1,0:T(8,128)(2,1)}, u32[]{:S(2)}, u32[]{:S(2)}) async-start(bf16[8,140,768]{2,1,0:T(8,128)(2,1)} %reshape.610), calls=%async_computation | async-start | bytes 3538944 | tf_op jit(solution)/shard_map/all_to_all | solution.py:182
  212.4 141.0 %all-gather.12.cloned.1.call-start = ((), (), s32[]{:S(2)}) async-start(), calls=%async_computation.15 | async-start | bytes 5898240 | tf_op jit(solution)/shard_map/all_gather | solution.py:109
  284.6 146.3 %copy-start.87 = (bf16[768,16]{0,1:T(8,128)(2,1)}, bf16[768,16]{0,1:T(8,128)(2,1)S(1)}, u32[]{:S(2)}) copy-start(bf16[768,16]{0,1:T(8,128)(2,1)S(1)} %reshape.663) | copy-start | bytes 73732
  293.8 198.9 %copy-start.210 = (f32[8]{0:T(128)}, f32[8]{0:T(128)S(1)}, u32[]{:S(2)}) copy-start(f32[8]{0:T(128)S(1)} %get-tuple-element.140) | copy-start | bytes 100
  300.2 192.9 %copy-start.99 = (f32[896,16]{0,1:T(8,128)}, f32[896,16]{0,1:T(8,128)S(1)}, u32[]{:S(2)}) copy-start(f32[896,16]{0,1:T(8,128)S(1)} %get-tuple-element.161) | copy-start | bytes 172036
  300.3 192.9 %copy-start.183 = (f32[896]{0:T(1024)}, f32[896]{0:T(1024)S(1)}, u32[]{:S(2)}) copy-start(f32[896]{0:T(1024)S(1)} %get-tuple-element.136) | copy-start | bytes 10756
  300.3 63.3 %all-to-all-start.2 = ((bf16[8,140,768]{2,1,0:T(8,128)(2,1)}), bf16[8,140,768]{2,1,0:T(8,128)(2,1)S(1)}, u32[]{:S(2)}, u32[]{:S(2)}) async-start(bf16[8,140,768]{2,1,0:T(8,128)(2,1)} %reshape.624), calls=%async_computation.2 | async-start | bytes 3538944 | tf_op jit(solution)/shard_map/all_to_all | solution.py:182
  363.6 61.3 %all-to-all-start.1 = ((bf16[8,140,768]{2,1,0:T(8,128)(2,1)}), bf16[8,140,768]{2,1,0:T(8,128)(2,1)}, u32[]{:S(2)}, u32[]{:S(2)}) async-start(bf16[8,140,768]{2,1,0:T(8,128)(2,1)} %fusion.136), calls=%async_computation.1 | async-start | bytes 3538944 | tf_op jit(solution)/shard_map/all_to_all | solution.py:189
  380.1 32.9 %copy-start.22 = (f32[8,140,3072]{2,1,0:T(8,128)}, f32[8,140,3072]{2,1,0:T(8,128)S(1)}, u32[]{:S(2)}) copy-start(f32[8,140,3072]{2,1,0:T(8,128)S(1)} %get-tuple-element.168) | copy-start | bytes 41287684
  424.9 47.8 %all-to-all-start.3 = ((bf16[8,140,768]{2,1,0:T(8,128)(2,1)}), bf16[8,140,768]{2,1,0:T(8,128)(2,1)}, u32[]{:S(2)}, u32[]{:S(2)}) async-start(bf16[8,140,768]{2,1,0:T(8,128)(2,1)} %fusion.139), calls=%async_computation.3 | async-start | bytes 3538944 | tf_op jit(solution)/shard_map/all_to_all | solution.py:189
  430.8 61.5 %copy-start.115 = (f32[896,8]{0,1:T(8,128)}, f32[896,8]{0,1:T(8,128)S(1)}, u32[]{:S(2)}) copy-start(f32[896,8]{0,1:T(8,128)S(1)} %get-tuple-element.163) | copy-start | bytes 86020
  430.9 61.5 %copy-start.175 = (f32[896]{0:T(1024)}, f32[896]{0:T(1024)S(1)}, u32[]{:S(2)}) copy-start(f32[896]{0:T(1024)S(1)} %get-tuple-element.162) | copy-start | bytes 10756
  430.9 61.4 %copy-start.161 = (f32[896]{0:T(1024)}, f32[896]{0:T(1024)S(1)}, u32[]{:S(2)}) copy-start(f32[896]{0:T(1024)S(1)} %fusion.201) | copy-start | bytes 10756
  431.2 62.5 %copy-start.101 = (f32[896,16]{0,1:T(8,128)}, f32[896,16]{0,1:T(8,128)S(1)}, u32[]{:S(2)}) copy-start(f32[896,16]{0,1:T(8,128)S(1)} %get-tuple-element.170) | copy-start | bytes 172036
  431.3 62.5 %copy-start.185 = (f32[896]{0:T(1024)}, f32[896]{0:T(1024)S(1)}, u32[]{:S(2)}) copy-start(f32[896]{0:T(1024)S(1)} %get-tuple-element.138) | copy-start | bytes 10756
  431.5 61.2 %copy-start.117 = (f32[896,8]{0,1:T(8,128)}, f32[896,8]{0,1:T(8,128)S(1)}, u32[]{:S(2)}) copy-start(f32[896,8]{0,1:T(8,128)S(1)} %get-tuple-element.172) | copy-start | bytes 86020
  431.5 61.2 %copy-start.177 = (f32[896]{0:T(1024)}, f32[896]{0:T(1024)S(1)}, u32[]{:S(2)}) copy-start(f32[896]{0:T(1024)S(1)} %get-tuple-element.171) | copy-start | bytes 10756
  431.6 61.2 %copy-start.163 = (f32[896]{0:T(1024)}, f32[896]{0:T(1024)S(1)}, u32[]{:S(2)}) copy-start(f32[896]{0:T(1024)S(1)} %fusion.202) | copy-start | bytes 10756
  439.1 53.3 %copy-start.191 = (f32[896]{0:T(1024)}, f32[896]{0:T(1024)S(1)}, u32[]{:S(2)}) copy-start(f32[896]{0:T(1024)S(1)} %get-tuple-element.164) | copy-start | bytes 10756
  441.6 34.7 %copy-start.104 = (f32[4,896]{1,0:T(4,128)S(1)}, f32[4,896]{1,0:T(4,128)}, u32[]{:S(2)}) copy-start(f32[4,896]{1,0:T(4,128)} %copy-done.103) | copy-start | bytes 43012
  441.6 34.7 %copy-start.137 = (f32[4,896]{1,0:T(4,128)S(1)}, f32[4,896]{1,0:T(4,128)}, u32[]{:S(2)}) copy-start(f32[4,896]{1,0:T(4,128)} %copy-done.136) | copy-start | bytes 43012
  441.6 35.3 %copy-start.106 = (f32[4,896]{1,0:T(4,128)S(1)}, f32[4,896]{1,0:T(4,128)}, u32[]{:S(2)}) copy-start(f32[4,896]{1,0:T(4,128)} %copy-done.105) | copy-start | bytes 43012
  441.6 35.3 %copy-start.139 = (f32[4,896]{1,0:T(4,128)S(1)}, f32[4,896]{1,0:T(4,128)}, u32[]{:S(2)}) copy-start(f32[4,896]{1,0:T(4,128)} %copy-done.138) | copy-start | bytes 43012
  441.6 35.9 %copy-start.108 = (f32[4,896]{1,0:T(4,128)S(1)}, f32[4,896]{1,0:T(4,128)}, u32[]{:S(2)}) copy-start(f32[4,896]{1,0:T(4,128)} %copy-done.107) | copy-start | bytes 43012
  443.0 37.7 %copy-start.29 = (bf16[896,768]{0,1:T(8,128)(2,1)S(1)}, bf16[896,768]{0,1:T(8,128)(2,1)}, u32[]{:S(2)}) copy-start(bf16[896,768]{0,1:T(8,128)(2,1)} %copy.262) | copy-start | bytes 4128772
  472.7 45.5 %all-to-all-start.4 = ((bf16[8,140,768]{2,1,0:T(8,128)(2,1)}), bf16[8,140,768]{2,1,0:T(8,128)(2,1)S(1)}, u32[]{:S(2)}, u32[]{:S(2)}) async-start(bf16[8,140,768]{2,1,0:T(8,128)(2,1)} %reshape.626), calls=%async_computation.4 | async-start | bytes 3538944 | tf_op jit(solution)/shard_map/all_to_all | solution.py:213
  518.2 46.5 %all-to-all-start.6 = ((bf16[8,140,768]{2,1,0:T(8,128)(2,1)}), bf16[8,140,768]{2,1,0:T(8,128)(2,1)}, u32[]{:S(2)}, u32[]{:S(2)}) async-start(bf16[8,140,768]{2,1,0:T(8,128)(2,1)} %reshape.640), calls=%async_computation.6 | async-start | bytes 3538944 | tf_op jit(solution)/shard_map/all_to_all | solution.py:213
  564.7 57.8 %all-to-all-start.5 = ((bf16[8,140,768]{2,1,0:T(8,128)(2,1)}), bf16[8,140,768]{2,1,0:T(8,128)(2,1)S(1)}, u32[]{:S(2)}, u32[]{:S(2)}) async-start(bf16[8,140,768]{2,1,0:T(8,128)(2,1)} %fusion.130), calls=%async_computation.5 | async-start | bytes 3538944 | tf_op jit(solution)/shard_map/all_to_all | solution.py:228
  568.3 422.3 %reduce-scatter.12.cloned.1.call-start = ((), (), s32[]{:S(2)}) async-start(), calls=%async_computation.19 | async-start | bytes 5898240 | tf_op jit(solution)/shard_map/reduce_scatter | solution.py:63
  622.4 47.3 %all-to-all-start.7 = ((bf16[8,140,768]{2,1,0:T(8,128)(2,1)}), bf16[8,140,768]{2,1,0:T(8,128)(2,1)}, u32[]{:S(2)}, u32[]{:S(2)}) async-start(bf16[8,140,768]{2,1,0:T(8,128)(2,1)} %fusion.133), calls=%async_computation.7 | async-start | bytes 3538944 | tf_op jit(solution)/shard_map/all_to_all | solution.py:228
  627.7 365.8 %reduce-scatter.10.cloned.1.call-start = ((), (), s32[]{:S(2)}) async-start(), calls=%async_computation.18 | async-start | bytes 5898240 | tf_op jit(solution)/shard_map/reduce_scatter | solution.py:60
  640.3 356.2 %reduce-scatter.8.cloned.1.call-start = ((), (), s32[]{:S(2)}) async-start(), calls=%async_computation.17 | async-start | bytes 2433024 | tf_op jit(solution)/shard_map/reduce_scatter | solution.py:313
  641.2 30.2 %copy-start.203 = (s32[896]{0:T(1024)S(1)}, s32[896]{0:T(1024)}, u32[]{:S(2)}) copy-start(s32[896]{0:T(1024)} %get-tuple-element.120) | copy-start | bytes 10756
  641.2 30.2 %copy-start.207 = (pred[896]{0:T(1024)(128)(4,1)S(1)}, pred[896]{0:T(1024)(128)(4,1)}, u32[]{:S(2)}) copy-start(pred[896]{0:T(1024)(128)(4,1)} %get-tuple-element.123) | copy-start | bytes 2692
  799.5 20.9 %slice-start.32 = ((s8[12845056]{0:T(1024)(128)(4,1)}), s8[262144]{0:T(1024)(128)(4,1)S(1)}, s32[]{:S(2)}) async-start(s8[12845056]{0:T(1024)(128)(4,1)} %bitcast.285), calls=%async_computation.52 | async-start | bytes 524288
  799.5 20.9 %slice-start.33 = ((s8[12845056]{0:T(1024)(128)(4,1)}), s8[4194304]{0:T(1024)(128)(4,1)S(1)}, s32[]{:S(2)}) async-start(s8[12845056]{0:T(1024)(128)(4,1)} %bitcast.285), calls=%async_computation.53 | async-start | bytes 8388608
  826.5 31.6 %slice-start.20 = ((s8[12845056]{0:T(1024)(128)(4,1)}), s8[4194304]{0:T(1024)(128)(4,1)S(1)}, s32[]{:S(2)}) async-start(s8[12845056]{0:T(1024)(128)(4,1)} %bitcast.279), calls=%async_computation.40 | async-start | bytes 8388608
  826.5 31.6 %slice-start.21 = ((s8[12845056]{0:T(1024)(128)(4,1)}), s8[4194304]{0:T(1024)(128)(4,1)S(1)}, s32[]{:S(2)}) async-start(s8[12845056]{0:T(1024)(128)(4,1)} %bitcast.279), calls=%async_computation.41 | async-start | bytes 8388608
  836.7 21.3 %slice-start.22 = ((s8[12845056]{0:T(1024)(128)(4,1)}), s8[4194304]{0:T(1024)(128)(4,1)S(1)}, s32[]{:S(2)}) async-start(s8[12845056]{0:T(1024)(128)(4,1)} %bitcast.279), calls=%async_computation.42 | async-start | bytes 8388608
  871.7 223.9 %reduce-scatter.6.cloned.1.call-start = ((), (), s32[]{:S(2)}) async-start(), calls=%async_computation.16 | async-start | bytes 7299072 | tf_op jit(solution)/shard_map/reduce_scatter | solution.py:312
  937.9 42.4 %copy-start.152 = (f32[896]{0:T(1024)S(1)}, f32[896]{0:T(1024)}, u32[]{:S(2)}) copy-start(f32[896]{0:T(1024)} %copy-done.151) | copy-start | bytes 10756
  (231 other events, 1278.4 us)
Sparse Core Ops, SparseCore 0:
  11.0 62.8 all-gather.5
  76.9 53.0 all-gather.7
  131.9 55.8 all-gather.9
  214.7 58.8 all-gather.11
  580.9 58.1 reduce-scatter.11
  641.9 57.1 reduce-scatter.9
  871.8 98.8 reduce-scatter.7
  976.9 118.6 reduce-scatter.5
where the time goes:
time: 1110 us; the launch traced here: 1100 us
  matrix products  400 us (36%)
  waiting for transfers between devices  183 us (16%)
  other arithmetic  176 us (16%)
  blocking collectives  152 us (14%)
  local copies, waits for them, and re-layouts  137 us (12%)
  starting transfers between devices  36.7 us (3%)
  between operations  17.7 us (2%)
    reduce_scatter x1, waiting for transfers between devices, per_device(): lax.psum_scatter(grad_qkv, ('dp', 'expert'), scatter_dimension=0, tiled=T...  99.1 us
    unnamed x2, blocking collectives  81.1 us
    all_gather x1, blocking collectives, dense_set(): lax.all_gather(route_proj, ('dp', 'expert'), axis=0, tiled=True)  71.4 us
    unnamed x562, local copies, waits for them, and re-layouts  70.6 us
    convert_element_type x2, other arithmetic, per_device(): inner_act = gelu_exact(pre_act).astype(jnp.bfloat16)  65.4 us
    convert_element_type x6, other arithmetic, per_device(): d_scores = (softmaxed * (d_probs - jnp.sum(softmaxed * d_probs, axis=-1,...  53.3 us
    dot_general x6, matrix products, per_device(): jnp.einsum('qhd,khd->hqk', d_heads, value_rows, preferred_element_type=jn...  41.6 us
    dot_general x2, matrix products, per_device(): jnp.einsum('scd,fd->scf', d_returned, wout_back, preferred_element_type=j...  37.4 us
  transfers between devices with their start and end apart: 16, of which 5 were waited for; matrix products, arithmetic and copies ran while one was open for 61% of the time, Pallas kernels for 0%

commit v1 on v0

v1 whole, which is shorter than its diff:
```python
import functools
import math

import jax
import jax.numpy as jnp
from jax import lax
from jax.experimental import pallas as pl
from jax.experimental.pallas import tpu as pltpu
from jax.sharding import PartitionSpec as P

D = 768
HEADS = 12
HEAD_DIM = 64
FF = 3072
ROUTE = 16
SEQ = 896
MB = 2

norm_eps = 1e-05
route_scale = 3.0
neg_big = -1e30
highest = lax.Precision.HIGHEST
bf16 = jnp.bfloat16
f32 = jnp.float32
NT = (((1,), (1,)), ((), ()))
TN = (((0,), (0,)), ((), ()))
NN = (((1,), (0,)), ((), ()))


def dot(a,b,dims=NN):
    return lax.dot_general(a,b,dims,preferred_element_type=f32)

def row_blocks(seq, block):
    return [(lo, min(lo+block, seq)) for lo in range(0, seq, block)]

def fwd_kernel(block, len_ref, q_ref, k_ref, v_ref, o_ref, lse_ref):
    seq=q_ref.shape[0]
    length=len_ref[0]
    lane=lax.broadcasted_iota(jnp.int32,(seq,128),1)
    place=lax.broadcasted_iota(jnp.int32,(seq,128),0)
    first=lane<64
    pad_bias=jnp.where(place<length,0.0,neg_big)
    q=q_ref[...].astype(f32)*0.125
    k=k_ref[...].astype(f32)
    v=v_ref[...].astype(f32)
    sides=[]
    for h in range(2):
        own=first if h==0 else jnp.logical_not(first)
        spare=lane==(64 if h==0 else 0)
        sides.append((
            jnp.where(own,q,jnp.where(spare,1.0,0.0)).astype(bf16),
            jnp.where(own,k,jnp.where(spare,pad_bias,0.0)).astype(bf16),
            jnp.where(own,v,1.0).astype(bf16)))
    for lo,hi in row_blocks(seq,block):
        n=hi-lo
        tri=lax.broadcasted_iota(jnp.int32,(n,n),1)<=lax.broadcasted_iota(jnp.int32,(n,n),0)
        outs=[]
        for qh,kh,vh in sides:
            s=dot(qh[lo:hi],kh[:hi],NT)
            edge=jnp.where(tri,s[:,lo:],neg_big)
            s=edge if lo==0 else jnp.concatenate([s[:,:lo],edge],axis=1)
            top=jnp.max(s,axis=1,keepdims=True)
            p=jnp.exp(s-top).astype(bf16)
            acc=dot(p,vh[:hi])
            total=pltpu.roll(acc,64,1)
            outs.append((acc/total, top+jnp.log(acc)))
        f=first[lo:hi]
        o_ref[lo:hi,:]=jnp.where(f,outs[0][0],outs[1][0]).astype(bf16)
        lse_ref[lo:hi,:]=jnp.where(f,outs[1][1],outs[0][1])

def attn_fwd(length, joined, block=256):
    seq=joined.shape[0]
    pairs=HEADS//2
    return pl.pallas_call(
        functools.partial(fwd_kernel,block),
        grid=(pairs,),
        in_specs=[pl.BlockSpec(memory_space=pltpu.SMEM),
            pl.BlockSpec((seq,128),lambda i:(0,i)),
            pl.BlockSpec((seq,128),lambda i:(0,i+pairs)),
            pl.BlockSpec((seq,128),lambda i:(0,i+2*pairs))],
        out_specs=[pl.BlockSpec((seq,128),lambda i:(0,i)),pl.BlockSpec((seq,128),lambda i:(0,i))],
        out_shape=[jax.ShapeDtypeStruct((seq,D),bf16),jax.ShapeDtypeStruct((seq,D),f32)],
        name="attn_fwd",
    )(length,joined,joined,joined)

def parts_of(x):
    hi=x.astype(bf16).astype(f32)
    mid=(x-hi).astype(bf16).astype(f32)
    lo=x-hi-mid
    return hi,mid,lo

def bwd_kernel(block, len_ref, q_ref, k_ref, v_ref, do_ref, o_ref, lse_ref, dq_ref, dk_ref, dv_ref, dk_acc, dv_acc):
    seq=q_ref.shape[0]
    length=len_ref[0]
    lane=lax.broadcasted_iota(jnp.int32,(seq,128),1)
    place=lax.broadcasted_iota(jnp.int32,(seq,128),0)
    first=lane<64
    pad_bias=jnp.where(place<length,0.0,neg_big)
    q=q_ref[...].astype(f32)*0.125
    k=k_ref[...].astype(f32)
    v=v_ref[...].astype(f32)
    do=do_ref[...].astype(f32)
    prod=do*o_ref[...].astype(f32)
    lse=lse_ref[...]
    sides=[]
    for h in range(2):
        own=first if h==0 else jnp.logical_not(first)
        a0=64 if h==0 else 0
        delta=jnp.sum(jnp.where(own,prod,0.0),axis=1,keepdims=True)
        l3=parts_of(lse); d3=parts_of(delta)
        is0=lane==a0; is1=lane==a0+1; is2=lane==a0+2; is3=lane==a0+3
        ones=jnp.where(is1|is2|is3,1.0,0.0)
        qa=jnp.where(own,q,jnp.where(is0,1.0,jnp.where(is1,-l3[0],jnp.where(is2,-l3[1],jnp.where(is3,-l3[2],0.0))))).astype(bf16)
        ka=jnp.where(own,k,jnp.where(is0,pad_bias,ones)).astype(bf16)
        da=jnp.where(own,do,jnp.where(is1,-d3[0],jnp.where(is2,-d3[1],jnp.where(is3,-d3[2],0.0)))).astype(bf16)
        va=jnp.where(own,v,ones).astype(bf16)
        sides.append((qa,ka,da,va,
            jnp.where(own,q,0.0).astype(bf16),
            jnp.where(own,k,0.0).astype(bf16),
            jnp.where(own,do,0.0).astype(bf16)))
    blocks=row_blocks(seq,block)
    for lo,hi in reversed(blocks):
        n=hi-lo
        tri=lax.broadcasted_iota(jnp.int32,(n,n),0)<=lax.broadcasted_iota(jnp.int32,(n,n),1)
        dq=None; dk=None; dv=None
        for qa,ka,da,va,qo,ko,do_o in sides:
            st=dot(ka[:hi],qa[lo:hi],NT)
            edge=jnp.where(tri,st[lo:],neg_big)
            st=edge if lo==0 else jnp.concatenate([st[:lo],edge],axis=0)
            pt=jnp.exp(st)
            dst=(pt*dot(va[:hi],da[lo:hi],NT)).astype(bf16)
            pb=pt.astype(bf16)
            t_v=dot(pb,do_o[lo:hi])
            t_k=dot(dst,qo[lo:hi])
            t_q=dot(dst,ko[:hi],TN)
            dv=t_v if dv is None else dv+t_v
            dk=t_k if dk is None else dk+t_k
            dq=t_q if dq is None else dq+t_q
        dq_ref[lo:hi,:]=(dq*0.125).astype(bf16)
        if (lo,hi)==blocks[-1]:
            dk_acc[...]=dk; dv_acc[...]=dv
        else:
            dk_acc[:hi,:]+=dk; dv_acc[:hi,:]+=dv
    dk_ref[...]=dk_acc[...].astype(bf16)
    dv_ref[...]=dv_acc[...].astype(bf16)

def attn_bwd(length, joined, d_mixed, mixed, lse, block=256):
    seq=joined.shape[0]
    pairs=HEADS//2
    col=pl.BlockSpec((seq,128),lambda i:(0,i))
    return pl.pallas_call(
        functools.partial(bwd_kernel,block),
        grid=(pairs,),
        in_specs=[pl.BlockSpec(memory_space=pltpu.SMEM),
            col,
            pl.BlockSpec((seq,128),lambda i:(0,i+pairs)),
            pl.BlockSpec((seq,128),lambda i:(0,i+2*pairs)),
            col,col,col],
        out_specs=[col,col,col],
        out_shape=[jax.ShapeDtypeStruct((seq,D),bf16)]*3,
        scratch_shapes=[pltpu.VMEM((seq,128),f32),pltpu.VMEM((seq,128),f32)],
        name="attn_bwd",
    )(length,joined,joined,joined,d_mixed,mixed,lse)


def layer_norm(values, gain_vec, shift_vec):
    center = values - jnp.mean(values, axis=-1, keepdims=True)
    spread = jnp.mean(center * center, axis=-1, keepdims=True)
    return center * lax.rsqrt(spread + norm_eps) * gain_vec + shift_vec


def unit_rows(values):
    norm_of = jnp.sqrt(jnp.sum(values * values, axis=-1, keepdims=True))
    return values / jnp.maximum(norm_of, 1.0)


def unit_back(values, unit, cotangent):
    norm_of = jnp.sqrt(jnp.sum(values * values, axis=-1, keepdims=True))
    along = jnp.sum(unit * cotangent, axis=-1, keepdims=True)
    return jnp.where(norm_of > 1.0, (cotangent - unit * along) / jnp.maximum(norm_of, 1.0), cotangent)


def gelu_exact(values):
    return jax.nn.gelu(values, approximate=False)


def swap(rows):
    return lax.all_to_all(rows, "expert", split_axis=0, concat_axis=0, tiled=True)


def sum_everywhere(value, sizes):
    for axis, size in sizes:
        step = 1
        while step < size:
            value = value + lax.ppermute(value, axis, [(i, i ^ step) for i in range(size)])
            step *= 2
    return value


def expert_work(arrived, upstream, win, wout, proj, embed, own):
    rows = arrived.shape[0] * arrived.shape[1]
    x = arrived.reshape(rows, D)
    up = upstream.reshape(rows, D)
    router_rows = dot(x, proj)
    unit_r = unit_rows(router_rows)
    unit_e = unit_rows(embed)
    chances = jax.nn.softmax(route_scale * jnp.dot(unit_r, unit_e.T, precision=highest), axis=-1)
    gate = jnp.sum(chances * own, axis=-1)
    pre_act = dot(x, win)
    inner_full, gelu_back = jax.vjp(gelu_exact, pre_act)
    inner = inner_full.astype(bf16)
    returned = dot(inner, wout).astype(bf16).astype(f32)
    up_wide = up.astype(f32)
    d_returned = (gate[:, None] * up_wide).astype(bf16)
    d_pre = gelu_back(dot(d_returned, wout, NT))[0].astype(bf16)
    d_gate = jnp.sum(up_wide * returned, axis=-1)
    d_logits = (route_scale * d_gate * gate)[:, None] * (own - chances)
    d_router = unit_back(
        router_rows, unit_r, jnp.dot(d_logits, unit_e, precision=highest)
    ).astype(bf16)
    d_embed = unit_back(embed, unit_e, jnp.dot(d_logits.T, unit_r, precision=highest))
    d_sent = (dot(d_pre, win, NT) + dot(d_router, proj, NT)).astype(bf16)
    y = (gate[:, None] * returned).astype(bf16)
    grads = (dot(x, d_pre, TN), dot(inner, d_returned, TN), dot(x, d_router, TN), d_embed)
    return y.reshape(arrived.shape), d_sent.reshape(arrived.shape), grads


def per_device(
    sizes,
    tokens,
    lengths,
    routes,
    slots,
    ln1_gain,
    ln1_bias,
    w_qkv,
    w_attn_out,
    ln2_gain,
    ln2_bias,
    route_proj,
    expert_embed,
    w_in,
    w_expert_out,
    out_grad,
):
    experts = expert_embed.shape[0]
    capacity = 5 * SEQ // (4 * experts)
    slot_cols = experts * capacity
    places = jnp.arange(SEQ, dtype=jnp.int32)
    columns = jnp.arange(slot_cols, dtype=jnp.int32)
    everyone = ("dp", "expert")

    vectors = jnp.stack([ln1_gain, ln1_bias, ln2_gain, ln2_bias], axis=1)
    share = jnp.concatenate([w_qkv, w_attn_out, route_proj, vectors], axis=1)
    share = jnp.pad(share, ((0, 0), (0, 3200 - share.shape[1])))
    dense = lax.all_gather(share, everyone, axis=0, tiled=True)
    qkv = dense[:, : 3 * D]
    attn_out = dense[:, 3 * D : 4 * D]
    proj = dense[:, 4 * D : 4 * D + ROUTE]
    norms = dense[:, 4 * D + ROUTE : 4 * D + ROUTE + 4].astype(f32).T
    gain_one, shift_one, gain_two, shift_two = [norms[i] for i in range(4)]
    win = lax.all_gather(w_in, "dp", axis=1, tiled=True)[0]
    wout = lax.all_gather(w_expert_out, "dp", axis=1, tiled=True)[0]
    own = (jnp.arange(experts) == lax.axis_index("expert")).astype(f32)[None, :]

    tables = []
    ups = []
    for at in range(MB):
        span = slice(at * SEQ, (at + 1) * SEQ)
        live = (places < lengths[at]) & (slots[span] < capacity)
        target = routes[span] * capacity + slots[span]
        table = ((target[:, None] == columns[None, :]) & live[:, None]).astype(bf16)
        tables.append(table)
        rows = dot(table, out_grad[span], TN).astype(bf16)
        ups.append(swap(rows.reshape(experts, capacity, D)))

    kept = []
    for at in range(MB):
        span = slice(at * SEQ, (at + 1) * SEQ)
        inputs = tokens[span].astype(f32)
        normed_one, back_one = jax.vjp(layer_norm, inputs, gain_one, shift_one)
        low_one = normed_one.astype(bf16)
        joined = dot(low_one, qkv).astype(bf16)
        mixed, lse = attn_fwd(lengths[at : at + 1], joined)
        hidden = inputs + dot(mixed, attn_out)
        normed_two, back_two = jax.vjp(layer_norm, hidden, gain_two, shift_two)
        low_two = normed_two.astype(bf16)
        rows = dot(tables[at], low_two, TN).astype(bf16)
        arrived = swap(rows.reshape(experts, capacity, D))
        kept.append((back_one, low_one, joined, mixed, lse, hidden, back_two, arrived))

    sent_back = []
    returned = []
    expert_grads = None
    for at in range(MB):
        y, d_sent, grads = expert_work(kept[at][-1], ups[at], win, wout, proj, expert_embed, own)
        sent_back.append(swap(d_sent))
        returned.append(swap(y))
        expert_grads = grads if at == 0 else tuple(a + b for a, b in zip(expert_grads, grads))
    grad_win, grad_wout, grad_proj, grad_embed = expert_grads
    win_out = lax.psum_scatter(grad_win[None].astype(bf16), "dp", scatter_dimension=1, tiled=True)
    wout_out = lax.psum_scatter(
        grad_wout[None].astype(bf16), "dp", scatter_dimension=1, tiled=True
    )
    embed_out = sum_everywhere(grad_embed, sizes)

    dense_grads = None
    in_grads = []
    outputs = []
    for at in range(MB):
        span = slice(at * SEQ, (at + 1) * SEQ)
        back_one, low_one, joined, mixed, lse, hidden, back_two, _ = kept[at]
        d_normed_two = dot(tables[at], sent_back[at].reshape(slot_cols, D))
        d_from_two, d_gain_two, d_shift_two = back_two(d_normed_two)
        d_hidden = out_grad[span].astype(f32) + d_from_two
        d_branch = d_hidden.astype(bf16)
        d_mixed = dot(d_branch, attn_out, NT).astype(bf16)
        parts = attn_bwd(lengths[at : at + 1], joined, d_mixed, mixed, lse)
        d_joined = jnp.concatenate(parts, axis=1)
        d_from_one, d_gain_one, d_shift_one = back_one(dot(d_joined, qkv, NT))
        in_grads.append((d_hidden + d_from_one).astype(bf16))
        grads = (
            dot(low_one, d_joined, TN),
            dot(mixed, d_branch, TN),
            d_gain_one,
            d_shift_one,
            d_gain_two,
            d_shift_two,
        )
        dense_grads = grads if at == 0 else tuple(a + b for a, b in zip(dense_grads, grads))
        outputs.append(
            (hidden + dot(tables[at], returned[at].reshape(slot_cols, D))).astype(bf16)
        )
    vectors = jnp.stack(dense_grads[2:], axis=1)
    packed = jnp.concatenate(
        [dense_grads[0], dense_grads[1], grad_proj, vectors], axis=1
    ).astype(bf16)
    packed = jnp.pad(packed, ((0, 0), (0, 3200 - packed.shape[1])))
    mine = lax.psum_scatter(packed, everyone, scatter_dimension=0, tiled=True).astype(f32)
    at = 4 * D + ROUTE
    return (
        jnp.concatenate(outputs, axis=0),
        jnp.concatenate(in_grads, axis=0),
        mine[:, at],
        mine[:, at + 1],
        mine[:, : 3 * D],
        mine[:, 3 * D : 4 * D],
        mine[:, at + 2],
        mine[:, at + 3],
        mine[:, 4 * D : at],
        embed_out,
        win_out.astype(f32),
        wout_out.astype(f32),
    )


def solution(mesh):
    rows = P(("dp", "expert"), None)
    flat = P(("dp", "expert"))
    bank = P("expert", "dp", None)
    sizes = (("expert", mesh.shape["expert"]), ("dp", mesh.shape["dp"]))
    return jax.shard_map(
        functools.partial(per_device, sizes),
        mesh=mesh,
        in_specs=(
            rows, flat, flat, flat, flat, flat, rows, rows, flat, flat, rows, P(), bank, bank, rows,
        ),
        out_specs=(
            rows, rows, flat, flat, rows, rows, flat, flat, rows, P(), bank, bank,
        ),
        check_vma=False,
    )
```

time: 1110 us -> 753 us (0.68)
  blocking collectives: 152 us -> 0 us
  other arithmetic: 176 us -> 42.9 us
  matrix products: 400 us -> 302 us
  Pallas kernels: 0 us -> 88.6 us
  waiting for transfers between devices: 183 us -> 131 us
  local copies, waits for them, and re-layouts: 137 us -> 113 us
  starting transfers between devices: 36.7 us -> 50.4 us
    convert_element_type x20 -> x11, other arithmetic: 137 us -> 20.4 us  [the longest x1 6.27 us: per_device(): in_grads.append((d_hidden + d_from_one).astype(bf16))]
    reduce_scatter x4 -> x2, waiting for transfers between devices: 99.1 us -> 0.01 us  [the longest x1 0.01 us: per_device(): lax.psum_scatter(grad_win[None].astype(bf16), 'dp', scatter_dimension=1,...]
    dot_general x80 -> x44, matrix products: 400 us -> 302 us  [the longest x38 300 us: dot(): return lax.dot_general(a, b, dims, preferred_element_type=f32)]
    pallas_call x0 -> x4, Pallas kernels: none -> 88.6 us  [the longest x2 47.3 us: attn_bwd(): pl.pallas_call(functools.partial(bwd_kernel, block), grid=(pairs,), in_sp...]
    unnamed x2 -> x0, blocking collectives: 81.1 us -> none
    all_gather x1 -> x0, blocking collectives: 71.4 us -> none  [dense_set(): lax.all_gather(route_proj, ('dp', 'expert'), axis=0, tiled=True)]
    ppermute x0 -> x5, waiting for transfers between devices: none -> 51 us  [sum_everywhere(): lax.ppermute(value, axis, [(i, i ^ step) for i in range(size)])]
    unnamed x562 -> x323, local copies, waits for them, and re-layouts: 70.6 us -> 32.4 us
  transfers between devices with their start and end apart: 16 -> 19, of which waited for: 5 -> 11; matrix products, arithmetic and copies ran while one was open for 61% -> 44% of each run, Pallas kernels for 0% -> 12%
where the time goes in v1:
time: 753 us; the launch traced here: 744 us
  matrix products  302 us (40%)
  waiting for transfers between devices  131 us (17%)
  local copies, waits for them, and re-layouts  113 us (15%)
  Pallas kernels  88.6 us (12%)
  starting transfers between devices  50.4 us (7%)
  other arithmetic  42.9 us (6%)
  between operations  16.4 us (2%)
    dot_general x38, matrix products, dot(): return lax.dot_general(a, b, dims, preferred_element_type=f32)  300 us
    all_to_all x8, waiting for transfers between devices, swap(): lax.all_to_all(rows, 'expert', split_axis=0, concat_axis=0, tiled=True)  69.8 us
    ppermute x5, waiting for transfers between devices, sum_everywhere(): lax.ppermute(value, axis, [(i, i ^ step) for i in range(size)])  51 us
    pallas_call x2, Pallas kernels, attn_bwd(): pl.pallas_call(functools.partial(bwd_kernel, block), grid=(pairs,), in_sp...  47.3 us
    all_to_all x8, starting transfers between devices, swap(): lax.all_to_all(rows, 'expert', split_axis=0, concat_axis=0, tiled=True)  41.7 us
    pallas_call x2, Pallas kernels, attn_fwd(): pl.pallas_call(functools.partial(fwd_kernel, block), grid=(pairs,), in_sp...  41.3 us
    unnamed x323, local copies, waits for them, and re-layouts  32.4 us
  transfers between devices with their start and end apart: 19, of which 11 were waited for; matrix products, arithmetic and copies ran while one was open for 44% of the time, Pallas kernels for 12%

profile of v1, /device:TPU:0, one launch (start us, length us, event | category | flops | bytes accessed | tf_op | source)
XLA Modules:
  0.0 744.2 jit_solution(12660684265804841067)
XLA Ops:
  22.7 6.4 all-to-all-start.4
  35.9 5.4 convolution_convert_fusion.2
  47.3 35.6 %all-to-all-done.4 = bf16[8,140,768]{2,1,0:T(8,128)(2,1)} async-done(((bf16[8,140,768]{2,1,0:T(8,128)(2,1)}), bf16[8,140,768]{2,1,0:T(8,128)(2,1)}, u32[]{:S(2)}, u32[]{:S(2)}) %all-to-all-start.4) | async-done | bytes 1720352 | tf_op jit(solution)/shard_map/all_to_all | solution.py:188
  82.9 4.5 all-to-all-start.6
  93.0 4.7 all-gather.4.cloned.1.call-done
  99.6 7.6 %convolution_convert_fusion.1.q_ref.k_ref.v_ref = bf16[896,2304]{1,0:T(8,128)(2,1)} fusion(bf16[768,3200]{1,0:T(8,128)(2,1)} %all-gather.4.cloned.1.call-done, bf16[896,768]{0,1:T(8,128)(2,1)S(1)} %copy.146, f32[768]{0:T(1024)S(1)} %get-tuple-element.90, f32[768]{0:T(1024)S(1)} %get-tuple-element.91, f32[896]{0:T(1024)S(1)} %fusion.148, ...), kind=kOutput, calls=%fused_computation.38 | convolution fusion | flops 3177086976 | bytes 9057280 | tf_op jit(solution)/shard_map/dot_general | solution.py:31
  107.2 20.8 %attn_fwd.2 = (bf16[896,768]{1,0:T(8,128)(2,1)}, f32[896,768]{1,0:T(8,128)}) custom-call(s32[1]{0:T(128)} %get-tuple-element.127.len_ref, bf16[896,2304]{1,0:T(8,128)(2,1)} %convolution_convert_fusion.1.q_ref.k_ref.v_ref, bf16[896,2304]{1,0:T(8,128)(2,1)} %convolution_convert_fusion.1.q_ref.k_ref.v_ref, ...), custom_call_target="tpu_custom_call" | custom-call | tf_op jit(solution)/shard_map/attn_fwd/pallas_call | solution.py:74
  137.1 7.6 %all-to-all-start = ((bf16[8,140,768]{2,1,0:T(8,128)(2,1)}), bf16[8,140,768]{2,1,0:T(8,128)(2,1)S(1)}, u32[]{:S(2)}, u32[]{:S(2)}) async-start(bf16[8,140,768]{2,1,0:T(8,128)(2,1)} %reshape.317), calls=%async_computation | async-start | bytes 3538944 | tf_op jit(solution)/shard_map/all_to_all | solution.py:188
  151.9 7.6 %convolution_convert_fusion.q_ref.k_ref.v_ref = bf16[896,2304]{1,0:T(8,128)(2,1)} fusion(bf16[768,3200]{1,0:T(8,128)(2,1)} %all-gather.4.cloned.1.call-done, bf16[896,768]{0,1:T(8,128)(2,1)S(1)} %copy.147, f32[896]{0:T(1024)S(1)} %fusion.150, f32[896]{0:T(1024)S(1)} %broadcast_multiply_fusion.1, f32[768]{0:T(1024)S(1)} %get-tuple-element.90, ...), kind=kOutput, calls=%fused_computation.37 | convolution fusion | flops 3177086976 | bytes 9057280 | tf_op jit(solution)/shard_map/dot_general | solution.py:31
  159.5 20.5 %attn_fwd.3 = (bf16[896,768]{1,0:T(8,128)(2,1)}, f32[896,768]{1,0:T(8,128)}) custom-call(s32[1]{0:T(128)} %get-tuple-element.128.len_ref, bf16[896,2304]{1,0:T(8,128)(2,1)} %convolution_convert_fusion.q_ref.k_ref.v_ref, bf16[896,2304]{1,0:T(8,128)(2,1)} %convolution_convert_fusion.q_ref.k_ref.v_ref, bf16[896,2304]{1,0:T(8,128)(2,1)} %convolution_convert_fusion.q_ref.k_ref.v_ref), custom_call_target="tpu_custom_call" | custom-call | tf_op jit(solution)/shard_map/attn_fwd/pallas_call | solution.py:74
  184.8 3.8 convolution_convert_fusion.4
  191.2 5.5 all-to-all-start.2
  198.5 39.1 %multiply_convert_fusion.1 = (bf16[1120,3072]{1,0:T(8,128)(2,1)}, f32[1120,3072]{1,0:T(8,128)}, f32[1120,3072]{1,0:T(8,128)}) fusion(bf16[1120,768]{1,0:T(8,128)(2,1)S(1)} %reshape.318, bf16[1,768,3072]{2,1,0:T(8,128)(2,1)} %all-gather.6.cloned.1.call-done), kind=kOutput, calls=%fused_computation.19 | convolution fusion | flops 5508464640 | bytes 40845312 | tf_op jit(solution)/shard_map/dot_general | solution.py:31
  252.4 18.7 %add_convert_fusion.1 = bf16[1120,3072]{1,0:T(8,128)(2,1)} fusion(f32[1120,3072]{1,0:T(8,128)} %get-tuple-element.106, bf16[1120,768]{1,0:T(8,128)(2,1)} %convert_element_type.203, f32[1120,3072]{1,0:T(8,128)} %get-tuple-element.142, bf16[1,3072,768]{2,1,0:T(8,128)(2,1)} %all-gather.8.cloned.1.call-done), kind=kOutput, calls=%fused_computation.5 | convolution fusion | flops 5332992000 | bytes 40845312 | tf_op jit(solution)/shard_map/dot_general | solution.py:31
  271.2 11.9 %fusion.179 = f32[768,3072]{1,0:T(8,128)} fusion(bf16[1120,768]{1,0:T(8,128)(2,1)S(1)} %reshape.318, bf16[1120,3072]{1,0:T(8,128)(2,1)} %add_convert_fusion.1), kind=kOutput, calls=%fused_computation.295 | convolution fusion | flops 5284823040 | bytes 18038784 | tf_op jit(solution)/shard_map/dot_general | solution.py:31
  286.4 38.8 %multiply_convert_fusion = (bf16[1120,3072]{1,0:T(8,128)(2,1)}, f32[1120,3072]{1,0:T(8,128)}, f32[1120,3072]{1,0:T(8,128)}) fusion(bf16[1120,768]{1,0:T(8,128)(2,1)S(1)} %reshape.322, bf16[1,768,3072]{2,1,0:T(8,128)(2,1)} %all-gather.6.cloned.1.call-done), kind=kOutput, calls=%fused_computation.6 | convolution fusion | flops 5508464640 | bytes 40845312 | tf_op jit(solution)/shard_map/dot_general | solution.py:31
  325.2 17.5 %add_convert_fusion = bf16[1120,3072]{1,0:T(8,128)(2,1)} fusion(f32[1120,3072]{1,0:T(8,128)} %get-tuple-element.108, bf16[1120,768]{1,0:T(8,128)(2,1)S(1)} %copy-done.24, f32[1120,3072]{1,0:T(8,128)} %get-tuple-element.131, bf16[1,3072,768]{2,1,0:T(8,128)(2,1)} %all-gather.8.cloned.1.call-done), kind=kOutput, calls=%fused_computation.4 | convolution fusion | flops 5332992000 | bytes 40845312 | tf_op jit(solution)/shard_map/dot_general | solution.py:31
  342.7 12.7 %fusion.27 = bf16[1,768,3072]{2,1,0:T(8,128)(2,1)} fusion(f32[768,3072]{1,0:T(8,128)} %fusion.179, bf16[1120,768]{1,0:T(8,128)(2,1)S(1)} %reshape.322, bf16[1120,3072]{1,0:T(8,128)(2,1)} %add_convert_fusion), kind=kOutput, calls=%fused_computation.54 | convolution fusion | flops 5289541632 | bytes 22757376 | tf_op jit(solution)/shard_map/dot_general | solution.py:31
  356.1 12.5 %fusion.49 = (f32[1120]{0:T(1024)S(1)}, bf16[1120,768]{1,0:T(8,128)(2,1)}) fusion(f32[1120,768]{1,0:T(8,128)} %reshape.331, f32[1120]{0:T(1024)S(1)} %copy-done.67, bf16[1120,3072]{1,0:T(8,128)(2,1)} %get-tuple-element.105, bf16[1,3072,768]{2,1,0:T(8,128)(2,1)} %all-gather.8.cloned.1.call-done), kind=kOutput, calls=%fused_computation.92 | convolution fusion | flops 5289982976 | bytes 16769792 | tf_op jit(solution)/shard_map/dot_general | solution.py:31
  368.6 11.7 %fusion.51 = (f32[1120]{0:T(1024)S(1)}, bf16[1120,768]{1,0:T(8,128)(2,1)}) fusion(f32[1120,768]{1,0:T(8,128)S(1)} %copy-done.20, f32[1120]{0:T(1024)S(1)} %copy-done.65, bf16[1120,3072]{1,0:T(8,128)(2,1)} %get-tuple-element.107, bf16[1,3072,768]{2,1,0:T(8,128)(2,1)} %all-gather.8.cloned.1.call-done), kind=kOutput, calls=%fused_computation.94 | convolution fusion | flops 5289982976 | bytes 16769792 | tf_op jit(solution)/shard_map/dot_general | solution.py:31
  381.1 5.8 fusion.19
  390.4 4.5 all-to-all-start.7
  395.4 9.4 %fusion.21 = f32[1120,768]{1,0:T(8,128)S(1)} fusion(bf16[1120,3072]{1,0:T(8,128)(2,1)} %add_convert_fusion.1, bf16[1,768,3072]{2,1,0:T(8,128)(2,1)} %all-gather.6.cloned.1.call-done), kind=kOutput, calls=%fused_computation.48 | convolution fusion | flops 5284823040 | bytes 15040512 | tf_op jit(solution)/shard_map/dot_general | solution.py:31
  411.3 12.1 %fusion.102 = f32[3072,768]{1,0:T(8,128)} fusion(bf16[1120,3072]{1,0:T(8,128)(2,1)} %get-tuple-element.105, f32[1120,768]{1,0:T(8,128)} %reshape.331, f32[1120]{0:T(1024)S(1)} %copy-done.67), kind=kOutput, calls=%fused_computation.162 | convolution fusion | flops 5286543360 | bytes 19763584 | tf_op jit(solution)/shard_map/dot_general | solution.py:31
  423.3 13.6 %all-to-all-done.7 = bf16[8,140,768]{2,1,0:T(8,128)(2,1)} async-done(((bf16[8,140,768]{2,1,0:T(8,128)(2,1)}), bf16[8,140,768]{2,1,0:T(8,128)(2,1)}, u32[]{:S(2)}, u32[]{:S(2)}) %all-to-all-start.7) | async-done | bytes 1720352 | tf_op jit(solution)/shard_map/all_to_all | solution.py:188
  445.1 12.7 %fusion.12 = bf16[1,3072,768]{2,1,0:T(8,128)(2,1)} fusion(f32[3072,768]{1,0:T(8,128)} %fusion.102, bf16[1120,3072]{1,0:T(8,128)(2,1)} %get-tuple-element.107, f32[1120,768]{1,0:T(8,128)} %reshape.332, f32[1120]{0:T(1024)} %copy-done.64), kind=kOutput, calls=%fused_computation.39 | convolution fusion | flops 5291261952 | bytes 24482176 | tf_op jit(solution)/shard_map/dot_general | solution.py:31
  463.1 19.4 %all-to-all-done.5 = bf16[8,140,768]{2,1,0:T(8,128)(2,1)S(1)} async-done(((bf16[8,140,768]{2,1,0:T(8,128)(2,1)}), bf16[8,140,768]{2,1,0:T(8,128)(2,1)S(1)}, u32[]{:S(2)}, u32[]{:S(2)}) %all-to-all-start.5) | async-done | bytes 1720352 | tf_op jit(solution)/shard_map/all_to_all | solution.py:188
  482.5 4.3 all-to-all-start.1
  488.4 5.3 fusion.176
  499.6 4.4 multiply_reduce_fusion.1
  509.3 4.5 convolution_convert_fusion.6.do_ref
  513.8 23.4 %attn_bwd.3 = (bf16[896,768]{1,0:T(8,128)(2,1)}, bf16[896,768]{1,0:T(8,128)(2,1)}, bf16[896,768]{1,0:T(8,128)(2,1)}) custom-call(s32[1]{0:T(128)} %get-tuple-element.128.len_ref, bf16[896,2304]{1,0:T(8,128)(2,1)} %convolution_convert_fusion.q_ref.k_ref.v_ref, bf16[896,2304]{1,0:T(8,128)(2,1)} %convolution_convert_fusion.q_ref.k_ref.v_ref, ...), custom_call_target="tpu_custom_call" | custom-call | tf_op jit(solution)/shard_map/attn_bwd/pallas_call | solution.py:151
  539.0 4.1 convolution_convert_fusion.7.do_ref
  543.1 23.9 %attn_bwd.2 = (bf16[896,768]{1,0:T(8,128)(2,1)}, bf16[896,768]{1,0:T(8,128)(2,1)}, bf16[896,768]{1,0:T(8,128)(2,1)}) custom-call(s32[1]{0:T(128)} %get-tuple-element.127.len_ref, bf16[896,2304]{1,0:T(8,128)(2,1)} %convolution_convert_fusion.1.q_ref.k_ref.v_ref, bf16[896,2304]{1,0:T(8,128)(2,1)} %convolution_convert_fusion.1.q_ref.k_ref.v_ref, ...), custom_call_target="tpu_custom_call" | custom-call | tf_op jit(solution)/shard_map/attn_bwd/pallas_call | solution.py:151
  572.1 7.7 %fusion.175 = (f32[768]{0:T(1024)S(1)}, f32[896,768]{1,0:T(8,128)S(1)}) fusion(bf16[896,2304]{1,0:T(8,128)(2,1)S(1)} %constant_dynamic-update-slice_fusion.3, bf16[768,3200]{1,0:T(8,128)(2,1)} %all-gather.4.cloned.1.call-done), kind=kOutput, calls=%fused_computation.291 | convolution fusion | flops 3171581184 | bytes 10423296 | tf_op jit(solution)/shard_map/dot_general | solution.py:31
  579.8 4.9 fusion.174
  593.8 4.0 fusion.69
  604.6 4.1 fusion.158
  608.7 5.8 add_convert_fusion.4
  614.5 8.5 %concatenate.24 = bf16[768,3092]{1,0:T(8,128)(2,1)} concatenate(bf16[768,2304]{1,0:T(8,128)(2,1)} %add_convert_fusion.4, bf16[768,768]{1,0:T(8,128)(2,1)} %add_convert_fusion.11, bf16[768,16]{1,0:T(8,128)(2,1)S(1)} %copy-done.37, bf16[768,1]{1,0:T(8,128)(2,1)} %add.246, bf16[768,1]{1,0:T(8,128)(2,1)S(1)} %add.247, bf16[768,1]{1,0:T(8,128)(2,1)S(1)} %add.248, bf16[768,1]{1,0:T(8,128)(2,1)S(1)} %add.249), dimensions={1} | concatenate | bytes 9498624 | tf_op jit(solution)/shard_map/concatenate | solution.py:335
  623.0 5.0 pad.9
  630.8 5.4 all-to-all-start.3
  640.3 25.5 %collective-permute-done.1 = f32[8,16]{1,0:T(8,128)S(1)} collective-permute-done((f32[8,16]{1,0:T(8,128)S(1)}, f32[8,16]{1,0:T(8,128)S(1)}, u32[]{:S(2)}, u32[]{:S(2)}) %collective-permute-start.1) | collective-permute-done | bytes 544 | tf_op jit(solution)/shard_map/ppermute | solution.py:195
  665.8 4.4 collective-permute-start.2
  670.3 19.0 %collective-permute-done.2 = f32[8,16]{1,0:T(8,128)S(1)} collective-permute-done((f32[8,16]{1,0:T(8,128)S(1)}, f32[8,16]{1,0:T(8,128)S(1)}, u32[]{:S(2)}, u32[]{:S(2)}) %collective-permute-start.2) | collective-permute-done | bytes 544 | tf_op jit(solution)/shard_map/ppermute | solution.py:195
  697.2 6.3 add_convert_fusion.6
  711.6 4.1 add_convert_fusion.9
  726.9 4.2 reduce-scatter.10.cloned.1.call-done
  (480 shorter events, 178.6 us)
Async XLA Ops:
  7.2 90.5 %all-gather.4.cloned.1.call-start = ((), (), s32[]{:S(2)}) async-start(), calls=%async_computation.11 | async-start | bytes 5068800 | tf_op jit(solution)/shard_map/all_gather | solution.py:256
  12.7 185.8 %all-gather.6.cloned.1.call-start = ((), (), s32[]{:S(2)}) async-start(), calls=%async_computation.12 | async-start | bytes 5898240 | tf_op jit(solution)/shard_map/all_gather | solution.py:262
  16.8 114.7 %copy-start.137 = (pred[896]{0:T(1024)(128)(4,1)}, pred[896]{0:T(1024)(128)(4,1)S(1)}, u32[]{:S(2)}) copy-start(pred[896]{0:T(1024)(128)(4,1)S(1)} %get-tuple-element.119) | copy-start | bytes 2692
  16.8 166.8 %copy-start.134 = (pred[896]{0:T(1024)(128)(4,1)}, pred[896]{0:T(1024)(128)(4,1)S(1)}, u32[]{:S(2)}) copy-start(pred[896]{0:T(1024)(128)(4,1)S(1)} %get-tuple-element.120) | copy-start | bytes 2692
  17.6 113.9 %copy-start.131 = (s32[896]{0:T(1024)}, s32[896]{0:T(1024)S(1)}, u32[]{:S(2)}) copy-start(s32[896]{0:T(1024)S(1)} %get-tuple-element.117) | copy-start | bytes 10756
  17.6 166.0 %copy-start.128 = (s32[896]{0:T(1024)}, s32[896]{0:T(1024)S(1)}, u32[]{:S(2)}) copy-start(s32[896]{0:T(1024)S(1)} %get-tuple-element.118) | copy-start | bytes 10756
  22.7 60.3 %all-to-all-start.4 = ((bf16[8,140,768]{2,1,0:T(8,128)(2,1)}), bf16[8,140,768]{2,1,0:T(8,128)(2,1)}, u32[]{:S(2)}, u32[]{:S(2)}) async-start(bf16[8,140,768]{2,1,0:T(8,128)(2,1)} %reshape.325), calls=%async_computation.4 | async-start | bytes 3538944 | tf_op jit(solution)/shard_map/all_to_all | solution.py:188
  29.0 223.4 %all-gather.8.cloned.1.call-start = ((), (), s32[]{:S(2)}) async-start(), calls=%async_computation.13 | async-start | bytes 5898240 | tf_op jit(solution)/shard_map/all_gather | solution.py:263
  33.6 94.3 %copy-start = (bf16[896,768]{0,1:T(8,128)(2,1)}, bf16[896,768]{0,1:T(8,128)(2,1)S(1)}, u32[]{:S(2)}) copy-start(bf16[896,768]{0,1:T(8,128)(2,1)S(1)} %copy.146) | copy-start | bytes 4128772
  35.9 144.1 %copy-start.2 = (bf16[896,768]{0,1:T(8,128)(2,1)}, bf16[896,768]{0,1:T(8,128)(2,1)S(1)}, u32[]{:S(2)}) copy-start(bf16[896,768]{0,1:T(8,128)(2,1)S(1)} %copy.147) | copy-start | bytes 4128772
  44.0 101.2 %copy-start.143 = (f32[8]{0:T(128)}, f32[8]{0:T(128)S(1)}, u32[]{:S(2)}) copy-start(f32[8]{0:T(128)S(1)} %multiply_reduce_fusion.14) | copy-start | bytes 100
  44.5 55.1 %copy-start.54 = (f32[896]{0:T(1024)}, f32[896]{0:T(1024)S(1)}, u32[]{:S(2)}) copy-start(f32[896]{0:T(1024)S(1)} %broadcast_multiply_fusion.3) | copy-start | bytes 10756
  45.6 53.9 %copy-start.78 = (f32[896]{0:T(1024)}, f32[896]{0:T(1024)S(1)}, u32[]{:S(2)}) copy-start(f32[896]{0:T(1024)S(1)} %fusion.148) | copy-start | bytes 10756
  82.9 54.2 %all-to-all-start.6 = ((bf16[8,140,768]{2,1,0:T(8,128)(2,1)}), bf16[8,140,768]{2,1,0:T(8,128)(2,1)}, u32[]{:S(2)}, u32[]{:S(2)}) async-start(bf16[8,140,768]{2,1,0:T(8,128)(2,1)} %reshape.328), calls=%async_computation.6 | async-start | bytes 3538944 | tf_op jit(solution)/shard_map/all_to_all | solution.py:188
  93.0 58.9 %copy-start.58 = (f32[896]{0:T(1024)}, f32[896]{0:T(1024)S(1)}, u32[]{:S(2)}) copy-start(f32[896]{0:T(1024)S(1)} %broadcast_multiply_fusion.1) | copy-start | bytes 10756
  99.5 52.4 %copy-start.56 = (f32[768]{0:T(1024)}, f32[768]{0:T(1024)S(1)}, u32[]{:S(2)}) copy-start(f32[768]{0:T(1024)S(1)} %get-tuple-element.91) | copy-start | bytes 9220
  99.5 52.3 %copy-start.126 = (f32[768]{0:T(1024)}, f32[768]{0:T(1024)S(1)}, u32[]{:S(2)}) copy-start(f32[768]{0:T(1024)S(1)} %get-tuple-element.90) | copy-start | bytes 9220
  99.6 84.1 %copy-start.72 = (f32[768]{0:T(1024)}, f32[768]{0:T(1024)S(1)}, u32[]{:S(2)}) copy-start(f32[768]{0:T(1024)S(1)} %get-tuple-element.88) | copy-start | bytes 9220
  137.1 54.1 %all-to-all-start = ((bf16[8,140,768]{2,1,0:T(8,128)(2,1)}), bf16[8,140,768]{2,1,0:T(8,128)(2,1)S(1)}, u32[]{:S(2)}, u32[]{:S(2)}) async-start(bf16[8,140,768]{2,1,0:T(8,128)(2,1)} %reshape.317), calls=%async_computation | async-start | bytes 3538944 | tf_op jit(solution)/shard_map/all_to_all | solution.py:188
  191.2 47.6 %all-to-all-start.2 = ((bf16[8,140,768]{2,1,0:T(8,128)(2,1)}), bf16[8,140,768]{2,1,0:T(8,128)(2,1)}, u32[]{:S(2)}, u32[]{:S(2)}) async-start(bf16[8,140,768]{2,1,0:T(8,128)(2,1)} %reshape.321), calls=%async_computation.2 | async-start | bytes 3538944 | tf_op jit(solution)/shard_map/all_to_all | solution.py:188
  196.8 524.4 %reduce-scatter.6.cloned.1.call-start = ((), (), s32[]{:S(2)}) async-start(), calls=%async_computation.14 | async-start | bytes 5898240 | tf_op jit(solution)/shard_map/reduce_scatter | solution.py:301
  198.4 72.7 %copy-start.16 = (bf16[1120,768]{1,0:T(8,128)(2,1)}, bf16[1120,768]{1,0:T(8,128)(2,1)S(1)}, u32[]{:S(2)}) copy-start(bf16[1120,768]{1,0:T(8,128)(2,1)S(1)} %reshape.318) | copy-start | bytes 5160964
  246.8 36.3 %copy-start.64 = (f32[1120]{0:T(1024)}, f32[1120]{0:T(1024)S(1)}, u32[]{:S(2)}) copy-start(f32[1120]{0:T(1024)S(1)} %get-tuple-element.100) | copy-start | bytes 13444
  286.4 38.8 %copy-start.24 = (bf16[1120,768]{1,0:T(8,128)(2,1)S(1)}, bf16[1120,768]{1,0:T(8,128)(2,1)}, u32[]{:S(2)}) copy-start(bf16[1120,768]{1,0:T(8,128)(2,1)} %convert_element_type.216) | copy-start | bytes 5160964
  356.1 24.8 %slice-start = ((s8[6881280]{0:T(1024)(128)(4,1)}), s8[4194304]{0:T(1024)(128)(4,1)S(1)}, s32[]{:S(2)}) async-start(s8[6881280]{0:T(1024)(128)(4,1)} %bitcast.80), calls=%async_computation.17 | async-start | bytes 8388608
  356.1 24.8 %slice-start.4 = ((s8[4718592]{0:T(1024)(128)(4,1)}), s8[4194304]{0:T(1024)(128)(4,1)S(1)}, s32[]{:S(2)}) async-start(s8[4718592]{0:T(1024)(128)(4,1)} %bitcast.88), calls=%async_computation.21 | async-start | bytes 8388608
  390.4 46.5 %all-to-all-start.7 = ((bf16[8,140,768]{2,1,0:T(8,128)(2,1)}), bf16[8,140,768]{2,1,0:T(8,128)(2,1)}, u32[]{:S(2)}, u32[]{:S(2)}) async-start(bf16[8,140,768]{2,1,0:T(8,128)(2,1)} %reshape.329), calls=%async_computation.7 | async-start | bytes 3538944 | tf_op jit(solution)/shard_map/all_to_all | solution.py:188
  436.9 45.5 %all-to-all-start.5 = ((bf16[8,140,768]{2,1,0:T(8,128)(2,1)}), bf16[8,140,768]{2,1,0:T(8,128)(2,1)S(1)}, u32[]{:S(2)}, u32[]{:S(2)}) async-start(bf16[8,140,768]{2,1,0:T(8,128)(2,1)} %reshape.326), calls=%async_computation.5 | async-start | bytes 3538944 | tf_op jit(solution)/shard_map/all_to_all | solution.py:188
  440.5 283.6 %reduce-scatter.8.cloned.1.call-start = ((), (), s32[]{:S(2)}) async-start(), calls=%async_computation.15 | async-start | bytes 5898240 | tf_op jit(solution)/shard_map/reduce_scatter | solution.py:302
  463.1 25.4 %copy-start.132 = (s32[896]{0:T(1024)S(1)}, s32[896]{0:T(1024)}, u32[]{:S(2)}) copy-start(s32[896]{0:T(1024)} %copy-done.131) | copy-start | bytes 10756
  463.1 25.4 %copy-start.138 = (pred[896]{0:T(1024)(128)(4,1)S(1)}, pred[896]{0:T(1024)(128)(4,1)}, u32[]{:S(2)}) copy-start(pred[896]{0:T(1024)(128)(4,1)} %copy-done.137) | copy-start | bytes 2692
  482.5 148.3 %all-to-all-start.1 = ((bf16[8,140,768]{2,1,0:T(8,128)(2,1)}), bf16[8,140,768]{2,1,0:T(8,128)(2,1)}, u32[]{:S(2)}, u32[]{:S(2)}) async-start(bf16[8,140,768]{2,1,0:T(8,128)(2,1)} %reshape.319), calls=%async_computation.1 | async-start | bytes 3538944 | tf_op jit(solution)/shard_map/all_to_all | solution.py:188
  486.8 244.3 %reduce-scatter.10.cloned.1.call-start = ((), (), s32[]{:S(2)}) async-start(), calls=%async_computation.16 | async-start | bytes 5068800
  507.8 29.5 %copy-start.5 = (f32[896,768]{0,1:T(8,128)}, f32[896,768]{0,1:T(8,128)S(1)}, u32[]{:S(2)}) copy-start(f32[896,768]{0,1:T(8,128)S(1)} %get-tuple-element.102) | copy-start | bytes 8257540
  543.1 23.9 %copy-start.31 = (bf16[896,768]{1,0:T(8,128)(2,1)S(1)}, bf16[896,768]{1,0:T(8,128)(2,1)}, u32[]{:S(2)}) copy-start(bf16[896,768]{1,0:T(8,128)(2,1)} %get-tuple-element.29) | copy-start | bytes 4128772
  630.7 66.4 %copy-start.121 = (f32[896]{0:T(1024)S(1)}, f32[896]{0:T(1024)}, u32[]{:S(2)}) copy-start(f32[896]{0:T(1024)} %get-tuple-element.85) | copy-start | bytes 10756
  630.7 66.4 %copy-start.116 = (f32[896]{0:T(1024)S(1)}, f32[896]{0:T(1024)}, u32[]{:S(2)}) copy-start(f32[896]{0:T(1024)} %get-tuple-element.87) | copy-start | bytes 10756
  630.7 66.4 %copy-start.80 = (f32[896]{0:T(1024)S(1)}, f32[896]{0:T(1024)}, u32[]{:S(2)}) copy-start(f32[896]{0:T(1024)} %copy-done.78) | copy-start | bytes 10756
  630.7 66.4 %copy-start.82 = (f32[896]{0:T(1024)S(1)}, f32[896]{0:T(1024)}, u32[]{:S(2)}) copy-start(f32[896]{0:T(1024)} %copy-done.81) | copy-start | bytes 10756
  630.7 66.4 %copy-start.84 = (f32[896]{0:T(1024)S(1)}, f32[896]{0:T(1024)}, u32[]{:S(2)}) copy-start(f32[896]{0:T(1024)} %copy-done.83) | copy-start | bytes 10756
  630.8 66.4 %copy-start.94 = (f32[896]{0:T(1024)S(1)}, f32[896]{0:T(1024)}, u32[]{:S(2)}) copy-start(f32[896]{0:T(1024)} %copy-done.93) | copy-start | bytes 10756
  630.8 66.4 %copy-start.97 = (f32[896]{0:T(1024)S(1)}, f32[896]{0:T(1024)}, u32[]{:S(2)}) copy-start(f32[896]{0:T(1024)} %copy-done.95) | copy-start | bytes 10756
  630.8 78.3 %all-to-all-start.3 = ((bf16[8,140,768]{2,1,0:T(8,128)(2,1)}), bf16[8,140,768]{2,1,0:T(8,128)(2,1)}, u32[]{:S(2)}, u32[]{:S(2)}) async-start(bf16[8,140,768]{2,1,0:T(8,128)(2,1)} %reshape.323), calls=%async_computation.3 | async-start | bytes 3538944 | tf_op jit(solution)/shard_map/all_to_all | solution.py:188
  637.1 1.3 collective-permute-start
  638.4 27.4 %collective-permute-start.1 = (f32[8,16]{1,0:T(8,128)S(1)}, f32[8,16]{1,0:T(8,128)S(1)}, u32[]{:S(2)}, u32[]{:S(2)}) collective-permute-start(f32[8,16]{1,0:T(8,128)S(1)} %add.239), channel_id=1, source_target_pairs={{0,2},{1,3},{2,0},{3,1},{4,6},{5,7},{6,4},{7,5},{8,10},{9,11},{10,... | collective-permute-start | bytes 1544 | tf_op jit(solution)/shard_map/ppermute | solution.py:195
  665.8 23.5 %collective-permute-start.2 = (f32[8,16]{1,0:T(8,128)S(1)}, f32[8,16]{1,0:T(8,128)S(1)}, u32[]{:S(2)}, u32[]{:S(2)}) collective-permute-start(f32[8,16]{1,0:T(8,128)S(1)} %add.240), channel_id=1, source_target_pairs={{0,4},{1,5},{2,6},{3,7},{4,0},{5,1},{6,2},{7,3},{8,12},{9,13},{10,... | collective-permute-start | bytes 1544 | tf_op jit(solution)/shard_map/ppermute | solution.py:195
  689.3 3.6 collective-permute-start.3
  692.9 3.6 collective-permute-start.4
  (126 other events, 553.5 us)
Sparse Core Ops, SparseCore 0:
  12.8 84.8 all-gather.3
  99.5 59.7 all-gather.5
  161.2 56.9 all-gather.7
  355.6 56.2 reduce-scatter.5
  457.9 57.1 reduce-scatter.7
  628.1 102.9 reduce-scatter.9
